TPU v7x, 8 devices: a whole 2x2x1 slice. The times are simulated.
8 devices in a mesh: tp: 4 (over z, y, x), dp: 2 (over core).
Axes of the slice: x: 2, y: 2, z: 1, core: 2. Of those that a mesh axis runs over, the one named last changes fastest.
Arguments:
- x_in: bfloat16 [128, 3072], P(('dp', 'tp'))
- w_gate: bfloat16 [3072, 8192], P('dp', 'tp')
- w_up: bfloat16 [3072, 8192], P('dp', 'tp')
- w_down: bfloat16 [8192, 3072], P('tp', 'dp')
- grad_y: bfloat16 [128, 3072], P(('dp', 'tp'))
Outputs:
- output 1: bfloat16 [128, 3072], P(('dp', 'tp'))
- output 2: bfloat16 [128, 3072], P(('dp', 'tp'))
- output 3: float32 [3072, 8192], P('dp', 'tp')
- output 4: float32 [3072, 8192], P('dp', 'tp')
- output 5: float32 [8192, 3072], P('tp', 'dp')
All inputs are finite; a program needn't handle non-finite values.
Results may differ from a plain program's by a relative error of at most 0.001.
Values are sent between devices in bfloat16 or wider.
A program may use at most 1 GiB of HBM per device.

v0:
```python
import jax
import jax.numpy as jnp
from jax import lax
from jax.sharding import PartitionSpec as P


def solution(mesh):
    dp_size = mesh.shape["dp"]
    tp_size = mesh.shape["tp"]

    def spread_cols(rows_loc):
        tok_dev = rows_loc.shape[0]
        cols_mine = lax.all_to_all(rows_loc, "dp", 1, 0, tiled=True)
        col_width = cols_mine.shape[1]
        cols_mine = cols_mine.reshape(dp_size, tok_dev, col_width)
        gathered = lax.all_gather(cols_mine, "tp", axis=1)
        return cols_mine, gathered.reshape(dp_size * tp_size * tok_dev, col_width)

    def collect_rows(col_part, resid):
        tok_dev = resid.shape[1]
        col_width = col_part.shape[1]
        summed = lax.psum_scatter(col_part.reshape(dp_size, tp_size, tok_dev, col_width), "tp", scatter_dimension=1, tiled=True)
        summed = summed.reshape(dp_size, tok_dev, col_width) + resid.astype(jnp.float32)
        out_rows = lax.all_to_all(summed.astype(jnp.bfloat16), "dp", 0, 2, tiled=True)
        return out_rows.reshape(tok_dev, dp_size * col_width)

    def local_step(x_loc, wg_loc, wu_loc, wd_loc, gy_loc):
        x_mine, x_cols = spread_cols(x_loc)
        gate_pre = lax.psum_scatter(jnp.dot(x_cols, wg_loc, preferred_element_type=jnp.float32), "dp", scatter_dimension=0, tiled=True)
        up_pre = lax.psum_scatter(jnp.dot(x_cols, wu_loc, preferred_element_type=jnp.float32), "dp", scatter_dimension=0, tiled=True)
        sig_gate = jax.nn.sigmoid(gate_pre)
        silu_gate = gate_pre * sig_gate
        hidden = (silu_gate * up_pre).astype(jnp.bfloat16)
        hidden_all = lax.all_gather(hidden, "dp", axis=0, tiled=True)
        y_rows = collect_rows(jnp.dot(hidden_all, wd_loc, preferred_element_type=jnp.float32), x_mine)

        gy_mine, gy_cols = spread_cols(gy_loc)
        grad_h = lax.psum_scatter(jnp.einsum("nd,fd->nf", gy_cols, wd_loc, preferred_element_type=jnp.float32), "dp", scatter_dimension=0, tiled=True)
        grad_wd = jnp.einsum("nf,nd->fd", hidden_all, gy_cols, preferred_element_type=jnp.float32)
        silu_deriv = sig_gate * (1.0 + gate_pre * (1.0 - sig_gate))
        grad_gate = (grad_h * up_pre * silu_deriv).astype(jnp.bfloat16)
        grad_up = (grad_h * silu_gate).astype(jnp.bfloat16)
        gate_all = lax.all_gather(grad_gate, "dp", axis=0, tiled=True)
        up_all = lax.all_gather(grad_up, "dp", axis=0, tiled=True)
        grad_wg = jnp.einsum("nd,nf->df", x_cols, gate_all, preferred_element_type=jnp.float32)
        grad_wu = jnp.einsum("nd,nf->df", x_cols, up_all, preferred_element_type=jnp.float32)
        gx_part = (jnp.einsum("nf,df->nd", gate_all, wg_loc, preferred_element_type=jnp.float32)
                   + jnp.einsum("nf,df->nd", up_all, wu_loc, preferred_element_type=jnp.float32))
        gx_rows = collect_rows(gx_part, gy_mine)
        return y_rows, gx_rows, grad_wg, grad_wu, grad_wd

    row_spec = P(("dp", "tp"), None)
    up_spec = P("dp", "tp")
    down_spec = P("tp", "dp")
    return jax.shard_map(local_step, mesh=mesh,
                         in_specs=(row_spec, up_spec, up_spec, down_spec, row_spec),
                         out_specs=(row_spec, row_spec, up_spec, up_spec, down_spec),
                         check_vma=False)
```

profile of v0, /device:TPU:0, one launch (start us, length us, event | category | flops | bytes accessed | tf_op | source)
XLA Modules:
  0.0 148.0 jit_solution(15624192560605204592)
XLA Ops:
  7.2 0.9 copy.49
  8.1 4.1 %all_to_all.62 = bf16[16,2,1536]{2,0,1:T(8,128)(2,1)S(1)} all-to-all(bf16[16,2,1536]{2,0,1:T(8,128)(2,1)S(1)} %bitcast.85), channel_id=1, replica_groups=mesh['tp'=4,'dp'=2] {'dp'}, dimensions={1} | all-to-all | bytes 196608 | tf_op jit(solution)/shard_map/all_to_all | solution.py:13
  12.4 0.5 copy-done.4
  12.9 11.0 %all-gather = bf16[2,64,1536]{2,0,1:T(2,128)(2,1)S(1)} all-gather(bf16[2,16,1536]{2,0,1:T(2,128)(2,1)S(1)} %copy.29), channel_id=2, replica_groups=mesh['tp'=4,'dp'=2] {'tp'}, dimensions={1}, use_global_device_ids=true | all-gather | bytes 491520 | tf_op jit(solution)/shard_map/all_gather | solution.py:16
  23.9 4.7 %fusion.5 = f32[128,2048]{1,0:T(8,128)} fusion(bf16[128,1536]{1,0:T(8,128)(2,1)S(1)} %bitcast.71, bf16[1536,2048]{1,0:T(8,128)(2,1)} %param.6), kind=kOutput, calls=%fused_computation.16 | convolution fusion | flops 805306368 | bytes 7733248 | tf_op jit(solution)/shard_map/dot_general | solution.py:29
  28.8 4.7 %fusion.6 = f32[128,2048]{1,0:T(8,128)} fusion(bf16[128,1536]{1,0:T(8,128)(2,1)S(1)} %bitcast.72, bf16[1536,2048]{1,0:T(8,128)(2,1)} %param.7), kind=kOutput, calls=%fused_computation.17 | convolution fusion | flops 805306368 | bytes 7733248 | tf_op jit(solution)/shard_map/dot_general | solution.py:30
  33.6 3.8 %all_to_all.63 = bf16[16,2,1536]{2,0,1:T(8,128)(2,1)S(1)} all-to-all(bf16[16,2,1536]{2,0,1:T(8,128)(2,1)S(1)} %bitcast.86), channel_id=1, replica_groups=mesh['tp'=4,'dp'=2] {'dp'}, dimensions={1} | all-to-all | bytes 196608 | tf_op jit(solution)/shard_map/all_to_all | solution.py:13
  37.5 0.5 copy-done.6
  38.1 9.5 %all-gather.1 = bf16[2,64,1536]{2,0,1:T(2,128)(2,1)S(1)} all-gather(bf16[2,16,1536]{2,0,1:T(2,128)(2,1)S(1)} %copy.33), channel_id=3, replica_groups=mesh['tp'=4,'dp'=2] {'tp'}, dimensions={1}, use_global_device_ids=true | all-gather | bytes 491520 | tf_op jit(solution)/shard_map/all_gather | solution.py:16
  47.6 0.7 copy-done.2
  48.4 5.9 %fusion.8 = f32[128,2048]{1,0:T(8,128)} fusion(bf16[128,1536]{1,0:T(8,128)(2,1)S(1)} %bitcast.75, bf16[2048,1536]{1,0:T(8,128)(2,1)} %param.8), kind=kOutput, calls=%fused_computation.19 | convolution fusion | flops 805306368 | bytes 7733248 | tf_op jit(solution)/shard_map/nd,fd->nf/dot_general | solution.py:38
  54.4 0.6 dynamic-slice
  55.0 5.0 %reduce-scatter.10.cloned.1.call-done = f32[64,2048]{1,0:T(8,128)} async-done(((f32[128,2048]{1,0:T(8,128)}), f32[64,2048]{1,0:T(8,128)}) %reduce-scatter.10.cloned.1.call-update) | async-done | bytes 524304 | tf_op jit(solution)/shard_map/reduce_scatter | solution.py:38
  60.0 1.6 %multiply_convert_fusion = (bf16[64,2048]{1,0:T(8,128)(2,1)S(1)}, bf16[64,2048]{1,0:T(8,128)(2,1)S(1)}, bf16[64,2048]{1,0:T(8,128)(2,1)S(1)}) fusion(f32[64,2048]{1,0:T(8,128)} %reduce-scatter.10.cloned.1.call-done, f32[64,2048]{1,0:T(8,128)} %reduce-scatter.6.cloned.1.call-done, f32[64,2048]{1,0:T(8,128)} %reduce-scatter.8.cloned.1.call-done), kind=kLoop, calls=%fused_computation.3 | loop fusion | flops 1966080 | bytes 2359296 | tf_op jit(solution)/shard_map/convert_element_type | solution.py:42
  61.7 2.2 %all_gather.18 = bf16[128,2048]{1,0:T(8,128)(2,1)S(1)} all-gather(bf16[64,2048]{1,0:T(8,128)(2,1)S(1)} %get-tuple-element.33), channel_id=1, replica_groups=mesh['tp'=4,'dp'=2] {'dp'}, dimensions={0}, use_global_device_ids=true | all-gather | bytes 786432 | tf_op jit(solution)/shard_map/all_gather | solution.py:43
  63.9 5.2 %fusion.9 = f32[128,1536]{1,0:T(8,128)S(1)} fusion(bf16[128,2048]{1,0:T(8,128)(2,1)S(1)} %all_gather.18, bf16[1536,2048]{1,0:T(8,128)(2,1)} %param.6), kind=kOutput, calls=%fused_computation.20 | convolution fusion | flops 805306368 | bytes 7602176 | tf_op jit(solution)/shard_map/nf,df->nd/dot_general | solution.py:47
  69.1 2.2 %all_gather.19 = bf16[128,2048]{1,0:T(8,128)(2,1)S(1)} all-gather(bf16[64,2048]{1,0:T(8,128)(2,1)S(1)} %get-tuple-element.32), channel_id=1, replica_groups=mesh['tp'=4,'dp'=2] {'dp'}, dimensions={0}, use_global_device_ids=true | all-gather | bytes 786432 | tf_op jit(solution)/shard_map/all_gather | solution.py:44
  71.3 2.5 %all_gather.16 = bf16[128,2048]{1,0:T(8,128)(2,1)S(1)} all-gather(bf16[64,2048]{1,0:T(8,128)(2,1)S(1)} %get-tuple-element.34), channel_id=1, replica_groups=mesh['tp'=4,'dp'=2] {'dp'}, dimensions={0}, use_global_device_ids=true | all-gather | bytes 786432 | tf_op jit(solution)/shard_map/all_gather | solution.py:34
  73.8 1.9 %fusion.7 = f32[128,1536]{1,0:T(8,128)} fusion(bf16[128,2048]{1,0:T(8,128)(2,1)S(1)} %all_gather.16, bf16[2048,1536]{1,0:T(8,128)(2,1)S(1)} %bitcast.68), kind=kOutput, calls=%fused_computation.18 | convolution fusion | flops 805306368 | bytes 7602176 | tf_op jit(solution)/shard_map/dot_general | solution.py:35
  75.7 3.1 %convolution_add_fusion = f32[128,1536]{1,0:T(8,128)} fusion(f32[128,1536]{1,0:T(8,128)S(1)} %fusion.9, bf16[128,2048]{1,0:T(8,128)(2,1)S(1)} %all_gather.19, bf16[1536,2048]{1,0:T(8,128)(2,1)S(1)} %bitcast.70), kind=kOutput, calls=%fused_computation.2 | convolution fusion | flops 805502976 | bytes 8388608 | tf_op jit(solution)/shard_map/nf,df->nd/dot_general | solution.py:48
  78.8 6.6 %convolution_bitcast_fusion.1 = f32[1536,2048]{0,1:T(8,128)} fusion(bf16[128,2048]{1,0:T(8,128)(2,1)S(1)} %copy-done.1, bf16[128,1536]{1,0:T(8,128)(2,1)S(1)} %bitcast.73), kind=kOutput, calls=%fused_computation.1 | convolution fusion | flops 805306368 | bytes 13500416 | tf_op jit(solution)/shard_map/nd,nf->df/dot_general | solution.py:45
  85.4 12.6 %copy.36 = f32[1536,2048]{1,0:T(8,128)} copy(f32[1536,2048]{0,1:T(8,128)} %convolution_bitcast_fusion.1) | data formatting | bytes 25165824
  98.0 6.6 %convolution_bitcast_fusion = f32[1536,2048]{0,1:T(8,128)} fusion(bf16[128,2048]{1,0:T(8,128)(2,1)S(1)} %all_gather.19, bf16[128,1536]{1,0:T(8,128)(2,1)S(1)} %bitcast.74), kind=kOutput, calls=%fused_computation | convolution fusion | flops 805306368 | bytes 13500416 | tf_op jit(solution)/shard_map/nd,nf->df/dot_general | solution.py:46
  104.6 12.7 %copy.37 = f32[1536,2048]{1,0:T(8,128)} copy(f32[1536,2048]{0,1:T(8,128)} %convolution_bitcast_fusion) | data formatting | bytes 25165824
  117.3 6.6 %fusion.10 = f32[2048,1536]{1,0:T(8,128)} fusion(bf16[128,2048]{1,0:T(8,128)(2,1)S(1)} %all_gather.16, bf16[128,1536]{1,0:T(8,128)(2,1)S(1)} %bitcast.76), kind=kOutput, calls=%fused_computation.21 | convolution fusion | flops 805306368 | bytes 13500416 | tf_op jit(solution)/shard_map/nf,nd->fd/dot_general | solution.py:39
  123.9 5.3 %all-reduce.5.cloned.1.call-done = (f32[2,4,16,1536]{3,2,1,0:T(8,128)}, f32[2,4,16,1536]{3,2,1,0:T(8,128)}) async-done(((f32[2,4,16,1536]{3,2,1,0:T(8,128)}, f32[2,4,16,1536]{3,2,1,0:T(8,128)}), (f32[2,4,16,1536]{3,2,1,0:T(8,128)}, f32[2,4,16,1536]{3,2,1,0:T(8,128)})) %all-reduce.5.cloned.1.call-update) | async-done | bytes 1572880
  129.2 1.6 %fusion.2 = bf16[2,16,1536]{2,1,0:T(8,128)(2,1)S(1)} fusion(f32[2,4,16,1536]{3,2,1,0:T(8,128)} %get-tuple-element.31, u32[]{:T(128)} %bitcast.18, bf16[16,2,1536]{2,0,1:T(8,128)(2,1)S(1)} %copy-done.7), kind=kLoop, calls=%fused_computation.10 | loop fusion | flops 147456 | bytes 393220 | tf_op jit(solution)/shard_map/convert_element_type | solution.py:24
  130.8 3.8 %all_to_all.64 = bf16[2,16,1536]{2,1,0:T(8,128)(2,1)S(1)} all-to-all(bf16[2,16,1536]{2,1,0:T(8,128)(2,1)S(1)} %fusion.2), channel_id=1, replica_groups=mesh['tp'=4,'dp'=2] {'dp'}, dimensions={0} | all-to-all | bytes 196608 | tf_op jit(solution)/shard_map/all_to_all | solution.py:24
  134.7 0.7 copy.45
  135.4 1.6 %fusion.4 = bf16[2,16,1536]{2,1,0:T(8,128)(2,1)S(1)} fusion(f32[2,4,16,1536]{3,2,1,0:T(8,128)} %get-tuple-element.30, u32[]{:T(128)} %bitcast.18, bf16[16,2,1536]{2,0,1:T(8,128)(2,1)S(1)} %copy-done.5), kind=kLoop, calls=%fused_computation.13 | loop fusion | flops 147456 | bytes 393220 | tf_op jit(solution)/shard_map/convert_element_type | solution.py:24
  136.9 3.8 %all_to_all.65 = bf16[2,16,1536]{2,1,0:T(8,128)(2,1)S(1)} all-to-all(bf16[2,16,1536]{2,1,0:T(8,128)(2,1)S(1)} %fusion.4), channel_id=1, replica_groups=mesh['tp'=4,'dp'=2] {'dp'}, dimensions={0} | all-to-all | bytes 196608 | tf_op jit(solution)/shard_map/all_to_all | solution.py:24
  140.8 0.7 copy.44
  (44 shorter events, 0.8 us)
Async XLA Ops:
  7.2 47.8 %reduce-scatter.6.cloned.1.call-start = ((), (), s32[]{:S(2)}) async-start(), calls=%async_computation.7 | async-start | bytes 1572864 | tf_op jit(solution)/shard_map/reduce_scatter | solution.py:29
  12.3 0.6 copy-start.4
  28.7 4.9 %copy-start.8 = (bf16[16,3072]{1,0:T(8,128)(2,1)S(1)}, bf16[16,3072]{1,0:T(8,128)(2,1)}, u32[]{:S(2)}) copy-start(bf16[16,3072]{1,0:T(8,128)(2,1)} %param.9) | copy-start | bytes 294916
  28.7 26.3 %reduce-scatter.8.cloned.1.call-start = ((), (), s32[]{:S(2)}) async-start(), calls=%async_computation.8 | async-start | bytes 1572864 | tf_op jit(solution)/shard_map/reduce_scatter | solution.py:30
  33.5 20.8 %copy-start.9 = (u32[8]{0:T(128)S(1)}, u32[8]{0:T(128)}, u32[]{:S(2)}) copy-start(u32[8]{0:T(128)} %constant.4) | copy-start | bytes 100
  33.6 26.5 %reduce-scatter.10.cloned.1.call-start = ((), (), s32[]{:S(2)}) async-start(), calls=%async_computation.9 | async-start | bytes 1572864 | tf_op jit(solution)/shard_map/reduce_scatter | solution.py:38
  37.4 0.6 copy-start.6
  47.6 0.8 copy-start.2
  54.3 19.5 %slice-start = ((s8[6291456]{0:T(1024)(128)(4,1)}), s8[2097152]{0:T(1024)(128)(4,1)S(1)}, s32[]{:S(2)}) async-start(s8[6291456]{0:T(1024)(128)(4,1)} %bitcast.67), calls=%async_computation.11 | async-start | bytes 4194304
  54.3 74.9 %all-reduce.5.cloned.1.call-start = ((), (), s32[]{:S(2)}) async-start(), calls=%async_computation.10 | async-start | bytes 3145728
  63.9 7.4 %copy-start = (bf16[128,2048]{1,0:T(8,128)(2,1)}, bf16[128,2048]{1,0:T(8,128)(2,1)S(1)}, u32[]{:S(2)}) copy-start(bf16[128,2048]{1,0:T(8,128)(2,1)S(1)} %all_gather.18) | copy-start | bytes 1572868
  63.9 9.9 %slice-start.1 = ((s8[6291456]{0:T(1024)(128)(4,1)}), s8[4194304]{0:T(1024)(128)(4,1)S(1)}, s32[]{:S(2)}) async-start(s8[6291456]{0:T(1024)(128)(4,1)} %bitcast.67), calls=%async_computation.12 | async-start | bytes 8388608
  71.3 4.4 %slice-start.2 = ((s8[6291456]{0:T(1024)(128)(4,1)}), s8[4194304]{0:T(1024)(128)(4,1)S(1)}, s32[]{:S(2)}) async-start(s8[6291456]{0:T(1024)(128)(4,1)} %bitcast.69), calls=%async_computation.13 | async-start | bytes 8388608
  73.8 1.9 %slice-start.3 = ((s8[6291456]{0:T(1024)(128)(4,1)}), s8[2097152]{0:T(1024)(128)(4,1)S(1)}, s32[]{:S(2)}) async-start(s8[6291456]{0:T(1024)(128)(4,1)} %bitcast.69), calls=%async_computation.14 | async-start | bytes 4194304
  75.6 3.2 %copy-start.1 = (bf16[128,2048]{1,0:T(8,128)(2,1)S(1)}, bf16[128,2048]{1,0:T(8,128)(2,1)}, u32[]{:S(2)}) copy-start(bf16[128,2048]{1,0:T(8,128)(2,1)} %copy-done) | copy-start | bytes 1572868
  104.6 12.7 %copy-start.3 = (bf16[2,64,1536]{2,1,0:T(8,128)(2,1)S(1)}, bf16[2,64,1536]{2,1,0:T(8,128)(2,1)}, u32[]{:S(2)}) copy-start(bf16[2,64,1536]{2,1,0:T(8,128)(2,1)} %copy-done.2) | copy-start | bytes 1179652
  117.3 11.9 %copy-start.7 = (bf16[16,2,1536]{2,0,1:T(8,128)(2,1)S(1)}, bf16[16,2,1536]{2,0,1:T(8,128)(2,1)}, u32[]{:S(2)}) copy-start(bf16[16,2,1536]{2,0,1:T(8,128)(2,1)} %copy-done.6) | copy-start | bytes 294916
  117.3 18.1 %copy-start.5 = (bf16[16,2,1536]{2,0,1:T(8,128)(2,1)S(1)}, bf16[16,2,1536]{2,0,1:T(8,128)(2,1)}, u32[]{:S(2)}) copy-start(bf16[16,2,1536]{2,0,1:T(8,128)(2,1)} %copy-done.4) | copy-start | bytes 294916
Sparse Core Ops, SparseCore 0:
  28.8 5.6 reduce-scatter.5
  37.3 6.7 reduce-scatter.7
  54.4 5.5 reduce-scatter.9
  78.9 50.2 all-reduce.4
where the time goes:
time: 149 us; the launch traced here: 148 us
  matrix products  45.4 us (30%)
  blocking collectives  42.9 us (29%)
  local copies, waits for them, and re-layouts  30.5 us (20%)
  between operations  13.9 us (9%)
  waiting for transfers between devices  10.4 us (7%)
  other arithmetic  4.78 us (3%)
    unnamed x33, local copies, waits for them, and re-layouts  29.1 us
    all_gather x2, blocking collectives, spread_cols(): gathered = lax.all_gather(cols_mine, 'tp', axis=1)  20.5 us
    all_to_all x2, blocking collectives, spread_cols(): cols_mine = lax.all_to_all(rows_loc, 'dp', 1, 0, tiled=True)  7.93 us
    all_to_all x2, blocking collectives, collect_rows(): lax.all_to_all(summed.astype(jnp.bfloat16), 'dp', 0, 2, tiled=True)  7.59 us
    dot_general x1, matrix products, local_step(): jnp.einsum('nd,nf->df', x_cols, gate_all, preferred_element_type=jnp.floa...  6.6 us
    dot_general x1, matrix products, local_step(): jnp.einsum('nd,nf->df', x_cols, up_all, preferred_element_type=jnp.float32)  6.6 us
    dot_general x1, matrix products, local_step(): jnp.einsum('nf,nd->fd', hidden_all, gy_cols, preferred_element_type=jnp.f...  6.6 us
    dot_general x1, matrix products, local_step(): jnp.einsum('nd,fd->nf', gy_cols, wd_loc, preferred_element_type=jnp.float32)  5.91 us
  transfers between devices with their start and end apart: 4, of which 2 were waited for; matrix products, arithmetic and copies ran while one was open for 38% of the time, Pallas kernels for 0%

commit v1 on v0

v1 whole, which is shorter than its diff:
```python
import functools

import jax
import jax.numpy as jnp
from jax import lax
from jax.experimental import pallas as pl
from jax.experimental.pallas import tpu as pltpu
from jax.sharding import PartitionSpec as P

MESH = pl.DeviceIdType.MESH
F32 = jnp.float32
BF16 = jnp.bfloat16

NT = (((1,), (1,)), ((), ()))
TN = (((0,), (0,)), ((), ()))

FC = 512
DC = 512


def _front(x_hbm, wg_hbm, wu_hbm, wd_hbm, gy_hbm,
           y_ref, dx_ref, xc_out, gc_out, h_out, da_out, db_out,
           x_v, gy_v, wg, wu, wd, xc, gc,
           pa, pb, pg, ra, rb, rg, sd, h, da, db,
           yp, yr, dxp, dxr,
           w_sem, o_sem, xs, xrs, gs, grs, es, ers, ys, yrs, ds, drs):
    rows, d_full = x_v.shape
    tok, d_half = xc.shape
    ff = wg.shape[1]
    nf = ff // FC
    nd = d_half // DC
    t = lax.axis_index("tp")
    c = lax.axis_index("dp")
    ty, tx = t // 2, t % 2
    peers = []
    for kt in range(4):
        for kc in range(2):
            px = tx if kt % 2 == 0 else 1 - tx
            py = ty if kt // 2 == 0 else 1 - ty
            pc = c if kc == 0 else 1 - c
            peers.append((py * 2 + px, pc))
    order = (6, 7, 2, 3, 4, 5, 1)

    def dev(k):
        return {"tp": peers[k][0], "dp": peers[k][1]}

    def row_of(k):
        return pl.multiple_of((peers[k][1] * 4 + peers[k][0]) * rows, rows)

    def col_of(k):
        return pl.multiple_of(peers[k][1] * d_half, d_half)

    cx = pltpu.make_async_copy(x_hbm, x_v, w_sem.at[0])
    cg = pltpu.make_async_copy(gy_hbm, gy_v, w_sem.at[1])
    cw = [pltpu.make_async_copy(a, b, w_sem.at[2 + i])
          for i, (a, b) in enumerate(((wg_hbm, wg), (wu_hbm, wu), (wd_hbm, wd)))]
    cx.start()
    cg.start()
    for w in cw:
        w.start()

    barrier = pltpu.get_barrier_semaphore()
    for k in range(1, 8):
        pl.semaphore_signal(barrier, inc=1, device_id=dev(k), device_id_type=MESH)
    pl.semaphore_wait(barrier, 7)

    def remote(src, dst, ssem, rsem, k):
        return pltpu.make_async_remote_copy(src_ref=src, dst_ref=dst, send_sem=ssem, recv_sem=rsem,
                                            device_id=dev(k), device_id_type=MESH)

    def spread(own, cols, ssem, rsem):
        out = []
        for k in order:
            cp = remote(own.at[:, pl.ds(col_of(k), d_half)], cols.at[pl.ds(row_of(0), rows), :],
                        ssem.at[k], rsem.at[k], k)
            cp.start()
            out.append(cp)
        return out

    cx.wait()
    sx = spread(x_v, xc, xs, xrs)
    cg.wait()
    sg = spread(gy_v, gc, gs, grs)
    xc[pl.ds(row_of(0), rows), :] = x_v[:, pl.ds(col_of(0), d_half)]
    gc[pl.ds(row_of(0), rows), :] = gy_v[:, pl.ds(col_of(0), d_half)]

    cw[0].wait()
    cw[1].wait()
    for cp in sx:
        cp.wait_recv()
    outs = [pltpu.make_async_copy(xc, xc_out, o_sem.at[0])]
    outs[0].start()
    ex = []
    for j in range(nf):
        f = slice(j * FC, (j + 1) * FC)
        pa[j] = jnp.dot(xc[...], wg[:, f], preferred_element_type=F32)
        ea = remote(pa.at[j], ra.at[j], es.at[3 * j], ers.at[3 * j], 1)
        ea.start()
        pb[j] = jnp.dot(xc[...], wu[:, f], preferred_element_type=F32)
        eb = remote(pb.at[j], rb.at[j], es.at[3 * j + 1], ers.at[3 * j + 1], 1)
        eb.start()
        ex.append((ea, eb))

    rb_rows = 16

    for j in range(nf):
        f = slice(j * FC, (j + 1) * FC)
        ex[j][0].wait_recv()
        ex[j][1].wait_recv()

        def act(i, carry, j=j, f=f):
            r = pl.ds(pl.multiple_of(i * rb_rows, rb_rows), rb_rows)
            a = pa[j, r, :] + ra[j, r, :]
            b = pb[j, r, :] + rb[j, r, :]
            s = jax.nn.sigmoid(a)
            u = a * s
            h[r, f] = (u * b).astype(BF16)
            sd[j, r, :] = s * (1.0 + a * (1.0 - s))
            ra[j, r, :] = u
            rb[j, r, :] = b
            return carry

        lax.fori_loop(0, tok // rb_rows, act, 0)
    outs.append(pltpu.make_async_copy(h, h_out, o_sem.at[1]))
    outs[1].start()

    def reduce_rows(part, recv, n, ssem, rsem):
        out = []
        for k in order:
            cp = remote(part.at[pl.ds(row_of(k), rows), pl.ds(n * DC, DC)],
                        recv.at[k, :, pl.ds(n * DC, DC)],
                        ssem.at[k * nd + n], rsem.at[k * nd + n], k)
            cp.start()
            out.append(cp)
        return out

    cw[2].wait()
    sy = []
    for n in range(nd):
        yp[:, n * DC:(n + 1) * DC] = jnp.dot(h[...], wd[:, n * DC:(n + 1) * DC], preferred_element_type=F32)
        sy += reduce_rows(yp, yr, n, ys, yrs)

    for cp in sg:
        cp.wait_recv()
    outs.append(pltpu.make_async_copy(gc, gc_out, o_sem.at[2]))
    outs[2].start()
    eg = []
    for j in range(nf):
        pg[j] = lax.dot_general(gc[...], wd[j * FC:(j + 1) * FC, :], NT, preferred_element_type=F32)
        e = remote(pg.at[j], rg.at[j], es.at[3 * j + 2], ers.at[3 * j + 2], 1)
        e.start()
        eg.append(e)
    for j in range(nf):
        f = slice(j * FC, (j + 1) * FC)
        eg[j].wait_recv()

        def grad(i, carry, j=j, f=f):
            r = pl.ds(pl.multiple_of(i * rb_rows, rb_rows), rb_rows)
            g = pg[j, r, :] + rg[j, r, :]
            da[r, f] = (g * rb[j, r, :] * sd[j, r, :]).astype(BF16)
            db[r, f] = (g * ra[j, r, :]).astype(BF16)
            return carry

        lax.fori_loop(0, tok // rb_rows, grad, 0)
    outs.append(pltpu.make_async_copy(da, da_out, o_sem.at[3]))
    outs.append(pltpu.make_async_copy(db, db_out, o_sem.at[4]))
    outs[3].start()
    outs[4].start()

    sdx = []
    for n in range(nd):
        dxp[:, n * DC:(n + 1) * DC] = (
            lax.dot_general(da[...], wg[n * DC:(n + 1) * DC, :], NT, preferred_element_type=F32)
            + lax.dot_general(db[...], wu[n * DC:(n + 1) * DC, :], NT, preferred_element_type=F32))
        sdx += reduce_rows(dxp, dxr, n, ds, drs)

    def finish(own, part, recv, out_ref):
        for kc in range(2):
            cols = pl.ds(col_of(kc), d_half)
            if kc == 0:
                tot = part[pl.ds(row_of(0), rows), :] + recv[2] + recv[4] + recv[6]
            else:
                tot = recv[1] + recv[3] + recv[5] + recv[7]
            out_ref[:, cols] = (own[:, cols].astype(F32) + tot).astype(BF16)

    for cp in sy:
        cp.wait_recv()
    finish(x_v, yp, yr, y_ref)
    for cp in sdx:
        cp.wait_recv()
    finish(gy_v, dxp, dxr, dx_ref)

    for cp in sx + sg + sy + sdx + eg:
        cp.wait_send()
    for ea, eb in ex:
        ea.wait_send()
        eb.wait_send()
    for o in outs:
        o.wait()


def _grads(h, da, db, xc, gc, dwd_hbm, dwg_hbm, dwu_hbm, buf_d, buf_g, sem_d, sem_g):
    ff = h.shape[1]
    d_half = xc.shape[1]
    nb_d, tr_d = buf_d.shape[:2]
    nb_g, tr_g = buf_g.shape[:2]

    def run(lhs, rhs, out, buf, sem, n, tr, nb, start, prev_out):
        def step(i, carry):
            slot = lax.rem(i + start, nb)
            r = pl.multiple_of(i * tr, tr)

            def drain():
                pltpu.make_async_copy(buf.at[slot], prev_out.at[pl.ds(0, tr), :], sem.at[slot]).wait()

            if start >= nb:
                drain()
            else:
                pl.when(i + start >= nb)(drain)
            buf[slot] = lax.dot_general(lhs[:, pl.ds(r, tr)], rhs[...], TN, preferred_element_type=F32)
            pltpu.make_async_copy(buf.at[slot], out.at[pl.ds(r, tr), :], sem.at[slot]).start()
            return carry

        lax.fori_loop(0, n, step, 0)

    n_d = ff // tr_d
    n_g = d_half // tr_g
    run(h, gc, dwd_hbm, buf_d, sem_d, n_d, tr_d, nb_d, 0, dwd_hbm)
    run(xc, da, dwg_hbm, buf_g, sem_g, n_g, tr_g, nb_g, 0, dwg_hbm)
    run(xc, db, dwu_hbm, buf_g, sem_g, n_g, tr_g, nb_g, n_g, dwu_hbm)
    for s in range(nb_d):
        pltpu.make_async_copy(buf_d.at[s], dwd_hbm.at[pl.ds(0, tr_d), :], sem_d.at[s]).wait()
    for s in range(nb_g):
        pltpu.make_async_copy(buf_g.at[s], dwu_hbm.at[pl.ds(0, tr_g), :], sem_g.at[s]).wait()


def solution(mesh):
    def local_step(x, wg, wu, wd, gy):
        rows, d_full = x.shape
        d_half, ff = wg.shape
        tok = rows * 8
        nf = ff // FC
        nd = d_half // DC
        any_ = pl.BlockSpec(memory_space=pl.ANY)
        vm = pl.BlockSpec(memory_space=pltpu.VMEM)
        S = jax.ShapeDtypeStruct
        dma = pltpu.SemaphoreType.DMA
        part = pltpu.VMEM((nf, tok, FC), F32)
        y, dx, xc, gc, h, da, db = pl.pallas_call(
            _front,
            name="front",
            out_shape=(S((rows, d_full), BF16), S((rows, d_full), BF16),
                       S((tok, d_half), BF16), S((tok, d_half), BF16),
                       S((tok, ff), BF16), S((tok, ff), BF16), S((tok, ff), BF16)),
            in_specs=[any_] * 5,
            out_specs=(vm, vm) + (any_,) * 5,
            scratch_shapes=[
                pltpu.VMEM((rows, d_full), BF16), pltpu.VMEM((rows, d_full), BF16),
                pltpu.VMEM((d_half, ff), BF16), pltpu.VMEM((d_half, ff), BF16), pltpu.VMEM((ff, d_half), BF16),
                pltpu.VMEM((tok, d_half), BF16), pltpu.VMEM((tok, d_half), BF16),
                part, part, part, part, part, part, part,
                pltpu.VMEM((tok, ff), BF16), pltpu.VMEM((tok, ff), BF16), pltpu.VMEM((tok, ff), BF16),
                pltpu.VMEM((tok, d_half), F32), pltpu.VMEM((8, rows, d_half), F32),
                pltpu.VMEM((tok, d_half), F32), pltpu.VMEM((8, rows, d_half), F32),
                dma((5,)), dma((5,)), dma((8,)), dma((8,)), dma((8,)), dma((8,)),
                dma((3 * nf,)), dma((3 * nf,)),
                dma((8 * nd,)), dma((8 * nd,)), dma((8 * nd,)), dma((8 * nd,)),
            ],
            compiler_params=pltpu.CompilerParams(collective_id=0, has_side_effects=True,
                                                 vmem_limit_bytes=50 * 1024 * 1024),
        )(x, wg, wu, wd, gy)

        tr = 256
        dwd, dwg, dwu = pl.pallas_call(
            _grads,
            name="grads",
            out_shape=(S((ff, d_half), F32), S((d_half, ff), F32), S((d_half, ff), F32)),
            in_specs=[vm] * 5,
            out_specs=(any_, any_, any_),
            scratch_shapes=[pltpu.VMEM((8, tr, d_half), F32), pltpu.VMEM((6, tr, ff), F32),
                            dma((8,)), dma((6,))],
            compiler_params=pltpu.CompilerParams(vmem_limit_bytes=50 * 1024 * 1024),
        )(h, da, db, xc, gc)
        return y, dx, dwg, dwu, dwd

    row_spec = P(("dp", "tp"), None)
    up_spec = P("dp", "tp")
    down_spec = P("tp", "dp")
    return jax.shard_map(local_step, mesh=mesh,
                         in_specs=(row_spec, up_spec, up_spec, down_spec, row_spec),
                         out_specs=(row_spec, row_spec, up_spec, up_spec, down_spec),
                         check_vma=False)
```

time: 149 us -> 52.8 us (0.35)
  Pallas kernels: 0 us -> 48.9 us
  matrix products: 45.4 us -> 0 us
  blocking collectives: 42.9 us -> 0 us
  local copies, waits for them, and re-layouts: 30.5 us -> 3.06 us
  between operations: 13.9 us -> 0.66 us
  waiting for transfers between devices: 10.4 us -> 0 us
  other arithmetic: 4.78 us -> 0 us
    pallas_call x0 -> x2, Pallas kernels: none -> 48.9 us  [the longest x1 36.3 us: local_step(): pl.pallas_call(_front, name='front', out_shape=(S((rows, d_full), BF16),...]
    dot_general x9 -> x0, matrix products: 45.4 us -> none  [the longest x1 6.6 us: local_step(): jnp.einsum('nd,nf->df', x_cols, gate_all, preferred_element_type=jnp.floa...]
    all_gather x5 -> x0, blocking collectives: 27.3 us -> none  [the longest x2 20.5 us: spread_cols(): gathered = lax.all_gather(cols_mine, 'tp', axis=1)]
    unnamed x33 -> x6, local copies, waits for them, and re-layouts: 29.1 us -> 3.06 us
    all_to_all x4 -> x0, blocking collectives: 15.5 us -> none  [the longest x2 7.93 us: spread_cols(): cols_mine = lax.all_to_all(rows_loc, 'dp', 1, 0, tiled=True)]
    unnamed x5 -> x0, waiting for transfers between devices: 5.4 us -> none
    reduce_scatter x3 -> x0, waiting for transfers between devices: 5.02 us -> none  [the longest x1 5.02 us: local_step(): lax.psum_scatter(jnp.einsum('nd,fd->nf', gy_cols, wd_loc, preferred_eleme...]
    convert_element_type x3 -> x0, other arithmetic: 4.77 us -> none  [the longest x2 3.14 us: collect_rows(): summed.astype(jnp.bfloat16)]
  transfers between devices with their start and end apart: 4 -> 0, of which waited for: 2 -> 0; matrix products, arithmetic and copies ran while one was open for 38% -> 0% of each run, Pallas kernels for 0% -> 0%
where the time goes in v1:
time: 52.8 us; the launch traced here: 52.7 us
  Pallas kernels  48.9 us (93%)
  local copies, waits for them, and re-layouts  3.06 us (6%)
  between operations  0.66 us (1%)
    pallas_call x1, Pallas kernels, local_step(): pl.pallas_call(_front, name='front', out_shape=(S((rows, d_full), BF16),...  36.3 us
    pallas_call x1, Pallas kernels, local_step(): pl.pallas_call(_grads, name='grads', out_shape=(S((ff, d_half), F32), S((...  12.7 us
    unnamed x6, local copies, waits for them, and re-layouts  3.06 us

profile of v1, /device:TPU:0, one launch (start us, length us, event | category | flops | bytes accessed | tf_op | source)
XLA Modules:
  0.0 52.7 jit_solution(9420007681743783781)
XLA Ops:
  0.6 0.0 copy-start
  0.6 0.9 %copy-done = bf16[16,3072]{1,0:T(8,128)(2,1)S(1)} copy-done((bf16[16,3072]{1,0:T(8,128)(2,1)S(1)}, bf16[16,3072]{1,0:T(8,128)(2,1)}, u32[]{:S(2)}) %copy-start) | copy-done | bytes 98328
  1.5 0.0 copy-start.1
  1.5 0.9 %copy-done.1 = bf16[16,3072]{1,0:T(8,128)(2,1)S(1)} copy-done((bf16[16,3072]{1,0:T(8,128)(2,1)S(1)}, bf16[16,3072]{1,0:T(8,128)(2,1)}, u32[]{:S(2)}) %copy-start.1) | copy-done | bytes 98328
  2.4 36.3 %front.1 = (bf16[16,3072]{1,0:T(8,128)(2,1)S(1)}, bf16[16,3072]{1,0:T(8,128)(2,1)S(1)}, bf16[128,1536]{1,0:T(8,128)(2,1)S(1)}, bf16[128,1536]{1,0:T(8,128)(2,1)S...) custom-call(bf16[16,3072]{1,0:T(8,128)(2,1)S(1)} %copy-done, ...), custom_call_target="tpu_custom_call" | custom-call | tf_op jit(solution)/shard_map/front/pallas_call | solution.py:249
  38.7 12.7 %grads.1 = (f32[2048,1536]{1,0:T(8,128)}, f32[1536,2048]{1,0:T(8,128)}, f32[1536,2048]{1,0:T(8,128)}) custom-call(bf16[128,2048]{1,0:T(8,128)(2,1)S(1)} %get-tuple-element.17.h, bf16[128,2048]{1,0:T(8,128)(2,1)S(1)} %get-tuple-element.18.da, bf16[128,2048]{1,0:T(8,128)(2,1)S(1)} %get-tuple-element.19.db, bf16[128,1536]{1,0:T(8,128)(2,1)S(1)} %get-tuple-element.20.xc, ...), custom_call_target="tpu_custom_call" | custom-call | tf_op jit(solution)/shard_map/grads/pallas_call | solution.py:274
  51.4 0.6 %copy.12 = bf16[16,3072]{1,0:T(8,128)(2,1)} copy(bf16[16,3072]{1,0:T(8,128)(2,1)S(1)} %get-tuple-element.30) | data formatting | bytes 196608
  52.0 0.6 %copy.13 = bf16[16,3072]{1,0:T(8,128)(2,1)} copy(bf16[16,3072]{1,0:T(8,128)(2,1)S(1)} %get-tuple-element.31) | data formatting | bytes 196608
Async XLA Ops:
  0.6 0.9 %copy-start = (bf16[16,3072]{1,0:T(8,128)(2,1)S(1)}, bf16[16,3072]{1,0:T(8,128)(2,1)}, u32[]{:S(2)}) copy-start(bf16[16,3072]{1,0:T(8,128)(2,1)} %x_hbm.1) | copy-start | bytes 294916
  1.5 0.9 %copy-start.1 = (bf16[16,3072]{1,0:T(8,128)(2,1)S(1)}, bf16[16,3072]{1,0:T(8,128)(2,1)}, u32[]{:S(2)}) copy-start(bf16[16,3072]{1,0:T(8,128)(2,1)} %gy_hbm.1) | copy-start | bytes 294916
